TPU v7x, 32 devices: a whole 2x2x4 slice. The times are simulated.
32 devices in a mesh: section: 2 (over x), expert: 4 (over y, core), dp: 4 (over z).
Axes of the slice: x: 2, y: 2, z: 4, core: 2. Of those that a mesh axis runs over, the one named last changes fastest.
Arguments:
- arrivals: bfloat16 [2, 1024, 2048], P('section', ('expert', 'dp')), may hold values from -6 to 6
- fresh: bfloat16 [1, 1024, 2048], P(None, ('expert', 'dp')), may hold values from -6 to 6
- routes: int32 [2, 2, 1024, 6], P('section', None, ('expert', 'dp')), may hold values from 0 to 63, as said below
- gates: bfloat16 [2, 2, 1024, 6], P('section', None, ('expert', 'dp')), may hold values from 0.099609375 to 1
- cotangent: bfloat16 [2, 2, 1024, 2048], P('section', None, ('expert', 'dp')), may hold values from -0.3125 to 0.3125
- norm_gain: float32 [2, 2048], P('section'), may hold values from 0.5 to 1.5
- w_gate: bfloat16 [2, 1408, 2048], P('section', 'expert', 'dp'), may hold values from -0.125 to 0.125
- w_up: bfloat16 [2, 1408, 2048], P('section', 'expert', 'dp'), may hold values from -0.125 to 0.125
- w_down: bfloat16 [2, 1408, 2048], P('section', 'expert', 'dp'), may hold values from -0.15625 to 0.15625
Outputs:
- layer_out: bfloat16 [2, 2, 1024, 2048], P('section', None, ('expert', 'dp'))
- grad_down: float32 [2, 1408, 2048], P('section', 'expert', 'dp')
Inputs may be any that keep to these rules, and one draw needn't show every extreme that they name: `routes`: each token's 6 entries are different expert numbers.
All inputs are finite; a program needn't handle non-finite values.
Results may differ from a plain program's by a relative error of at most 0.0085.
Values may be sent and summed in bfloat16 or wider, within the bound.
A program may use at most 64 MiB of HBM per device.

v0:
```python
import jax
import jax.numpy as jnp
from jax import lax
from jax.sharding import PartitionSpec as P

SPLIT = 4
CAP = 12


def shifted_2(shard, axis, by):
    count = lax.axis_size(axis)
    pairs = [(i, i + by) for i in range(count) if 0 <= i + by < count]
    return lax.ppermute(shard, axis, pairs)


def local(arrivals, fresh, routes, gates, cotangent, norm_gain, w_gate, w_up, w_down):
    n_expert = lax.axis_size("expert")
    flight = n_expert // SPLIT
    section_index = lax.axis_index("section")
    tok_rows = arrivals.shape[1]
    model_width = arrivals.shape[2]
    step_count = routes.shape[1]
    gains = norm_gain[0]
    gate_local, up_local, down_local = (
        lax.all_gather(w_gate[0], "dp", axis=1, tiled=True),
        lax.all_gather(w_up[0], "dp", axis=1, tiled=True),
        lax.all_gather(w_down[0], "dp", axis=1, tiled=True),
    )
    hid_rows = gate_local.shape[0]
    slot_ids = jnp.arange(CAP, dtype=jnp.int32)
    expert_ids = jnp.arange(flight, dtype=jnp.int32)
    highest = lax.Precision.HIGHEST
    row_dims = (((0,), (0,)), ((), ()))

    def selection(step_index):
        routing = routes[0, step_index]
        weights = gates[0, step_index].astype(jnp.float32)
        matches = routing[:, :, None] == expert_ids[None, None, :]
        naming = jnp.any(matches, axis=1).astype(jnp.int32)
        shares = jnp.sum(jnp.where(matches, weights[:, :, None], 0.0), axis=1)
        places = jnp.cumsum(naming, axis=0) - naming
        chosen = (naming.T[:, None, :] == 1) & (places.T[:, None, :] == slot_ids[None, :, None])
        select = chosen.reshape(flight * CAP, tok_rows).astype(jnp.bfloat16)
        slot_gate = jnp.sum(jnp.where(chosen, shares.T[:, None, :], 0.0), axis=2).reshape(
            flight * CAP
        )
        counts = jnp.minimum(jnp.sum(naming, axis=0), CAP)
        return (select, slot_gate, counts)

    def fan_out(block_in):
        spread = jnp.broadcast_to(block_in[:, None], (flight, SPLIT) + block_in.shape[1:])
        return spread.reshape((n_expert,) + block_in.shape[1:])

    def pack_rows(select, values):
        rows = jnp.dot(select, values, preferred_element_type=jnp.float32).astype(jnp.bfloat16)
        return fan_out(rows.reshape(flight, CAP, model_width))

    picks = [selection(turn_num) for turn_num in range(step_count)]
    incoming = arrivals[0]
    grad_total = jnp.zeros((hid_rows, model_width), jnp.float32)
    outputs = []
    for turn_num in range(step_count):
        if turn_num > 0:
            shifted = shifted_2(outputs[-1], "section", 1)
            incoming = jnp.where(section_index == 0, fresh[turn_num - 1], shifted)
        floats = incoming.astype(jnp.float32)
        scale = lax.rsqrt(jnp.mean(floats * floats, axis=1, keepdims=True) + 0.5)
        normed = (floats * scale * gains[None, :]).astype(jnp.bfloat16)
        select, slot_gate, counts = picks[turn_num]
        send_tok = pack_rows(select, normed)
        send_cot = pack_rows(select, cotangent[0, turn_num])
        send_gate = fan_out(slot_gate.reshape(flight, CAP).astype(jnp.bfloat16))
        send_count = fan_out(counts)
        rows_tok, rows_cot, rows_gate, rows_count = (
            lax.all_to_all(send_tok, "expert", split_axis=0, concat_axis=0, tiled=True),
            lax.all_to_all(send_cot, "expert", split_axis=0, concat_axis=0, tiled=True),
            lax.all_to_all(send_gate, "expert", split_axis=0, concat_axis=0, tiled=True),
            lax.all_to_all(send_count, "expert", split_axis=0, concat_axis=0, tiled=True),
        )
        total_rows = n_expert * CAP
        flat_tok = rows_tok.reshape(total_rows, model_width)
        flat_cot = rows_cot.reshape(total_rows, model_width)
        flat_gate = rows_gate.reshape(total_rows)
        dims = (((1,), (1,)), ((), ()))
        gate_act = lax.dot_general(flat_tok, gate_local, dims, preferred_element_type=jnp.float32)
        up_act = lax.dot_general(flat_tok, up_local, dims, preferred_element_type=jnp.float32)
        hidden = (jax.nn.silu(gate_act) * up_act).astype(jnp.bfloat16)
        partial_value = jnp.dot(hidden, down_local, preferred_element_type=jnp.float32).astype(
            jnp.bfloat16
        )
        weighted = (hidden.astype(jnp.float32) * flat_gate.astype(jnp.float32)[:, None]).astype(
            jnp.bfloat16
        )
        expert_partial_value = partial_value
        grad_add = lax.dot_general(weighted, flat_cot, row_dims, preferred_element_type=jnp.float32)
        partial_value, grad_add = (
            expert_partial_value.reshape(n_expert, CAP, model_width),
            grad_add,
        )
        returned = lax.all_to_all(partial_value, "expert", split_axis=0, concat_axis=0, tiled=True)
        expert_out = jnp.sum(
            returned.reshape(flight, SPLIT, CAP, model_width).astype(jnp.float32), axis=1
        ).reshape(flight * CAP, model_width)
        mixing = select.astype(jnp.float32).T * slot_gate[None, :]
        mixture = jnp.dot(mixing, expert_out, precision=highest)
        result = (floats + mixture).astype(jnp.bfloat16)
        outputs.append(result)
        grad_total = grad_total + grad_add
    grad_part = lax.psum_scatter(grad_total, "dp", scatter_dimension=1, tiled=True)
    return (jnp.stack(outputs)[None], grad_part[None])


def solution(mesh):
    placed = (
        P("section", ("expert", "dp"), None),
        P(None, ("expert", "dp"), None),
        P("section", None, ("expert", "dp"), None),
        P("section", None, ("expert", "dp"), None),
        P("section", None, ("expert", "dp"), None),
        P("section", None),
        P("section", "expert", "dp"),
        P("section", "expert", "dp"),
        P("section", "expert", "dp"),
    )
    return jax.shard_map(
        local,
        mesh=mesh,
        in_specs=placed,
        out_specs=(P("section", None, ("expert", "dp"), None), P("section", "expert", "dp")),
        check_vma=False,
    )
```

profile of v0, /device:TPU:0, one launch (start us, length us, event | category | flops | bytes accessed | tf_op | source)
XLA Modules:
  0.0 242.2 jit_solution(11923948752257591277)
XLA Ops:
  9.4 0.8 compare_reduce_fusion
  10.5 1.1 fusion.26
  11.9 0.7 reshape.550
  12.7 4.3 %all-to-all-start = ((bf16[4,12,2048]{2,1,0:T(8,128)(2,1)}), bf16[4,12,2048]{2,1,0:T(8,128)(2,1)S(1)}, u32[]{:S(2)}, u32[]{:S(2)}) async-start(bf16[4,12,2048]{2,1,0:T(8,128)(2,1)} %reshape.550), calls=%async_computation | async-start | bytes 524288 | tf_op jit(solution)/shard_map/all_to_all | solution.py:75
  17.7 5.3 %all-to-all-done = bf16[4,12,2048]{2,1,0:T(8,128)(2,1)S(1)} async-done(((bf16[4,12,2048]{2,1,0:T(8,128)(2,1)}), bf16[4,12,2048]{2,1,0:T(8,128)(2,1)S(1)}, u32[]{:S(2)}, u32[]{:S(2)}) %all-to-all-start) | async-done | bytes 196640 | tf_op jit(solution)/shard_map/all_to_all | solution.py:75
  23.0 24.1 %all-gather.7.cloned.1.call-done = bf16[1,352,2048]{2,1,0:T(8,128)(2,1)} async-done(((bf16[1,352,512]{2,1,0:T(8,128)(2,1)}), bf16[1,352,2048]{2,1,0:T(8,128)(2,1)}) %all-gather.7.cloned.1.call-update) | async-done | bytes 1441808 | tf_op jit(solution)/shard_map/all_gather | solution.py:25
  47.0 1.9 fusion.11
  49.0 33.5 %all-gather.9.cloned.1.call-done = bf16[1,352,2048]{2,1,0:T(8,128)(2,1)} async-done(((bf16[1,352,512]{2,1,0:T(8,128)(2,1)}), bf16[1,352,2048]{2,1,0:T(8,128)(2,1)}) %all-gather.9.cloned.1.call-update) | async-done | bytes 1441808 | tf_op jit(solution)/shard_map/all_gather | solution.py:26
  82.5 1.9 fusion.22
  84.4 33.4 %all-gather.11.cloned.1.call-done = bf16[1,352,2048]{2,1,0:T(8,128)(2,1)} async-done(((bf16[1,352,512]{2,1,0:T(8,128)(2,1)}), bf16[1,352,2048]{2,1,0:T(8,128)(2,1)}) %all-gather.11.cloned.1.call-update) | async-done | bytes 1441808 | tf_op jit(solution)/shard_map/all_gather | solution.py:27
  117.8 1.7 convolution_convert_fusion.1
  119.6 0.8 reshape.552
  120.3 3.4 %all-to-all-start.1 = ((bf16[4,12,2048]{2,1,0:T(8,128)(2,1)}), bf16[4,12,2048]{2,1,0:T(8,128)(2,1)S(1)}, u32[]{:S(2)}, u32[]{:S(2)}) async-start(bf16[4,12,2048]{2,1,0:T(8,128)(2,1)} %reshape.552), calls=%async_computation.1 | async-start | bytes 524288 | tf_op jit(solution)/shard_map/all_to_all | solution.py:100
  123.9 5.8 %all-to-all-done.1 = bf16[4,12,2048]{2,1,0:T(8,128)(2,1)S(1)} async-done(((bf16[4,12,2048]{2,1,0:T(8,128)(2,1)}), bf16[4,12,2048]{2,1,0:T(8,128)(2,1)S(1)}, u32[]{:S(2)}, u32[]{:S(2)}) %all-to-all-start.1) | async-done | bytes 196640 | tf_op jit(solution)/shard_map/all_to_all | solution.py:100
  130.3 3.2 %all-to-all-start.4 = ((bf16[4,1,12]{2,1,0:T(2,128)(2,1)}), bf16[4,1,12]{2,1,0:T(2,128)(2,1)S(1)}, u32[]{:S(2)}, u32[]{:S(2)}) async-start(bf16[4,1,12]{2,1,0:T(2,128)(2,1)} %reshape.557), calls=%async_computation.4 | async-start | bytes 4096 | tf_op jit(solution)/shard_map/all_to_all | solution.py:77
  134.2 3.0 %all-to-all-done.4 = bf16[4,1,12]{2,1,0:T(2,128)(2,1)S(1)} async-done(((bf16[4,1,12]{2,1,0:T(2,128)(2,1)}), bf16[4,1,12]{2,1,0:T(2,128)(2,1)S(1)}, u32[]{:S(2)}, u32[]{:S(2)}) %all-to-all-start.4) | async-done | bytes 128 | tf_op jit(solution)/shard_map/all_to_all | solution.py:77
  137.8 3.2 %all-to-all-start.6 = ((bf16[4,1,12]{2,1,0:T(2,128)(2,1)}), bf16[4,1,12]{2,1,0:T(2,128)(2,1)S(1)}, u32[]{:S(2)}, u32[]{:S(2)}) async-start(bf16[4,1,12]{2,1,0:T(2,128)(2,1)} %reshape.560), calls=%async_computation.6 | async-start | bytes 4096 | tf_op jit(solution)/shard_map/all_to_all | solution.py:77
  141.0 3.5 %collective-permute-start = (bf16[64,2048]{1,0:T(8,128)(2,1)S(1)}, bf16[64,2048]{1,0:T(8,128)(2,1)S(1)}, u32[]{:S(2)}, u32[]{:S(2)}) collective-permute-start(bf16[64,2048]{1,0:T(8,128)(2,1)S(1)} %fusion), channel_id=1, source_target_pairs={{0,16},{1,17},{2,18},{3,19},{4,20},{5,21},{6,22},{7,23},{8,24},{9,... | collective-permute-start | bytes 786440 | tf_op jit(solution)/shard_map/ppermute | solution.py:13
  145.4 3.4 %all-to-all-start.5 = ((bf16[4,12,2048]{2,1,0:T(8,128)(2,1)}), bf16[4,12,2048]{2,1,0:T(8,128)(2,1)S(1)}, u32[]{:S(2)}, u32[]{:S(2)}) async-start(bf16[4,12,2048]{2,1,0:T(8,128)(2,1)} %reshape.558), calls=%async_computation.5 | async-start | bytes 524288 | tf_op jit(solution)/shard_map/all_to_all | solution.py:76
  149.0 5.8 %all-to-all-done.5 = bf16[4,12,2048]{2,1,0:T(8,128)(2,1)S(1)} async-done(((bf16[4,12,2048]{2,1,0:T(8,128)(2,1)}), bf16[4,12,2048]{2,1,0:T(8,128)(2,1)S(1)}, u32[]{:S(2)}, u32[]{:S(2)}) %all-to-all-start.5) | async-done | bytes 196640 | tf_op jit(solution)/shard_map/all_to_all | solution.py:76
  155.5 3.4 %all-to-all-start.7 = ((bf16[4,12,2048]{2,1,0:T(8,128)(2,1)}), bf16[4,12,2048]{2,1,0:T(8,128)(2,1)S(1)}, u32[]{:S(2)}, u32[]{:S(2)}) async-start(bf16[4,12,2048]{2,1,0:T(8,128)(2,1)} %reshape.561), calls=%async_computation.7 | async-start | bytes 524288 | tf_op jit(solution)/shard_map/all_to_all | solution.py:76
  159.8 5.1 %all-to-all-done.7 = bf16[4,12,2048]{2,1,0:T(8,128)(2,1)S(1)} async-done(((bf16[4,12,2048]{2,1,0:T(8,128)(2,1)}), bf16[4,12,2048]{2,1,0:T(8,128)(2,1)S(1)}, u32[]{:S(2)}, u32[]{:S(2)}) %all-to-all-start.7) | async-done | bytes 196640 | tf_op jit(solution)/shard_map/all_to_all | solution.py:76
  166.1 0.7 reshape.554
  166.8 3.4 %all-to-all-start.2 = ((bf16[4,12,2048]{2,1,0:T(8,128)(2,1)}), bf16[4,12,2048]{2,1,0:T(8,128)(2,1)S(1)}, u32[]{:S(2)}, u32[]{:S(2)}) async-start(bf16[4,12,2048]{2,1,0:T(8,128)(2,1)} %reshape.554), calls=%async_computation.2 | async-start | bytes 524288 | tf_op jit(solution)/shard_map/all_to_all | solution.py:75
  170.3 1.4 fusion.43
  171.7 4.5 %all-to-all-done.2 = bf16[4,12,2048]{2,1,0:T(8,128)(2,1)S(1)} async-done(((bf16[4,12,2048]{2,1,0:T(8,128)(2,1)}), bf16[4,12,2048]{2,1,0:T(8,128)(2,1)S(1)}, u32[]{:S(2)}, u32[]{:S(2)}) %all-to-all-start.2) | async-done | bytes 196640 | tf_op jit(solution)/shard_map/all_to_all | solution.py:75
  176.3 2.0 fusion.9
  178.9 2.2 convolution_add_fusion
  181.2 1.3 copy-done
  182.9 8.4 %all_to_all.42 = bf16[4,12,2048]{2,1,0:T(8,128)(2,1)S(1)} all-to-all(bf16[4,12,2048]{2,1,0:T(8,128)(2,1)S(1)} %reshape.556), channel_id=1, replica_groups=mesh['section'=2,'expert'=4,'dp'=4] {'expert'}, dimensions={0} | all-to-all | bytes 393216 | tf_op jit(solution)/shard_map/all_to_all | solution.py:100
  192.0 0.8 maximum_bitcast_fusion
  192.9 42.8 %reduce-scatter.2.cloned.1.call-done = f32[352,512]{1,0:T(8,128)} async-done(((f32[352,2048]{1,0:T(8,128)}), f32[352,512]{1,0:T(8,128)}) %reduce-scatter.2.cloned.1.call-update) | async-done | bytes 720912 | tf_op jit(solution)/shard_map/reduce_scatter | solution.py:109
  (78 shorter events, 11.0 us)
Async XLA Ops:
  7.2 10.1 %copy-start.10 = (s32[1,2,64,6]{2,1,3,0:T(2,128)S(1)}, s32[1,2,64,6]{2,1,3,0:T(2,128)}, u32[]{:S(2)}) copy-start(s32[1,2,64,6]{2,1,3,0:T(2,128)} %param.11) | copy-start | bytes 9220
  7.2 4.5 %copy-start.2 = (bf16[1,64,2048]{2,1,0:T(8,128)(2,1)S(1)}, bf16[1,64,2048]{2,1,0:T(8,128)(2,1)}, u32[]{:S(2)}) copy-start(bf16[1,64,2048]{2,1,0:T(8,128)(2,1)} %param.9) | copy-start | bytes 786436
  7.2 4.5 %copy-start.13 = (f32[1,2048]{1,0:T(1,128)S(1)}, f32[1,2048]{1,0:T(1,128)}, u32[]{:S(2)}) copy-start(f32[1,2048]{1,0:T(1,128)} %param.14) | copy-start | bytes 24580
  7.2 10.1 %copy-start.11 = (bf16[1,2,64,6]{2,1,3,0:T(2,128)(2,1)S(1)}, bf16[1,2,64,6]{2,1,3,0:T(2,128)(2,1)}, u32[]{:S(2)}) copy-start(bf16[1,2,64,6]{2,1,3,0:T(2,128)(2,1)} %param.12) | copy-start | bytes 4612
  7.2 39.8 %all-gather.7.cloned.1.call-start = ((), (), s32[]{:S(2)}) async-start(), calls=%async_computation.10 | async-start | bytes 1802240 | tf_op jit(solution)/shard_map/all_gather | solution.py:25
  7.9 74.5 %all-gather.9.cloned.1.call-start = ((), (), s32[]{:S(2)}) async-start(), calls=%async_computation.11 | async-start | bytes 1802240 | tf_op jit(solution)/shard_map/all_gather | solution.py:26
  8.7 109.1 %all-gather.11.cloned.1.call-start = ((), (), s32[]{:S(2)}) async-start(), calls=%async_computation.12 | async-start | bytes 1802240 | tf_op jit(solution)/shard_map/all_gather | solution.py:27
  12.7 10.3 %all-to-all-start = ((bf16[4,12,2048]{2,1,0:T(8,128)(2,1)}), bf16[4,12,2048]{2,1,0:T(8,128)(2,1)S(1)}, u32[]{:S(2)}, u32[]{:S(2)}) async-start(bf16[4,12,2048]{2,1,0:T(8,128)(2,1)} %reshape.550), calls=%async_computation | async-start | bytes 524288 | tf_op jit(solution)/shard_map/all_to_all | solution.py:75
  84.4 35.9 %copy-start.8 = (bf16[48,352]{1,0:T(8,128)(2,1)}, bf16[48,352]{1,0:T(8,128)(2,1)S(1)}, u32[]{:S(2)}) copy-start(bf16[48,352]{1,0:T(8,128)(2,1)S(1)} %fusion.22) | copy-start | bytes 101380
  84.4 39.3 %copy-start.7 = (bf16[1,2,64,2048]{3,2,1,0:T(8,128)(2,1)S(1)}, bf16[1,2,64,2048]{3,2,1,0:T(8,128)(2,1)}, u32[]{:S(2)}) copy-start(bf16[1,2,64,2048]{3,2,1,0:T(8,128)(2,1)} %param.13) | copy-start | bytes 1572868
  120.3 9.4 %all-to-all-start.1 = ((bf16[4,12,2048]{2,1,0:T(8,128)(2,1)}), bf16[4,12,2048]{2,1,0:T(8,128)(2,1)S(1)}, u32[]{:S(2)}, u32[]{:S(2)}) async-start(bf16[4,12,2048]{2,1,0:T(8,128)(2,1)} %reshape.552), calls=%async_computation.1 | async-start | bytes 524288 | tf_op jit(solution)/shard_map/all_to_all | solution.py:100
  130.3 6.9 %all-to-all-start.4 = ((bf16[4,1,12]{2,1,0:T(2,128)(2,1)}), bf16[4,1,12]{2,1,0:T(2,128)(2,1)S(1)}, u32[]{:S(2)}, u32[]{:S(2)}) async-start(bf16[4,1,12]{2,1,0:T(2,128)(2,1)} %reshape.557), calls=%async_computation.4 | async-start | bytes 4096 | tf_op jit(solution)/shard_map/all_to_all | solution.py:77
  134.2 30.7 %copy-start.5 = (bf16[64,2048]{1,0:T(8,128)(2,1)}, bf16[64,2048]{1,0:T(8,128)(2,1)S(1)}, u32[]{:S(2)}) copy-start(bf16[64,2048]{1,0:T(8,128)(2,1)S(1)} %fusion) | copy-start | bytes 786436
  137.8 6.9 %all-to-all-start.6 = ((bf16[4,1,12]{2,1,0:T(2,128)(2,1)}), bf16[4,1,12]{2,1,0:T(2,128)(2,1)S(1)}, u32[]{:S(2)}, u32[]{:S(2)}) async-start(bf16[4,1,12]{2,1,0:T(2,128)(2,1)} %reshape.560), calls=%async_computation.6 | async-start | bytes 4096 | tf_op jit(solution)/shard_map/all_to_all | solution.py:77
  141.0 24.0 %copy-start.9 = (bf16[1,64,2048]{2,1,0:T(8,128)(2,1)S(1)}, bf16[1,64,2048]{2,1,0:T(8,128)(2,1)}, u32[]{:S(2)}) copy-start(bf16[1,64,2048]{2,1,0:T(8,128)(2,1)} %param.10) | copy-start | bytes 786436
  141.0 23.9 %collective-permute-start = (bf16[64,2048]{1,0:T(8,128)(2,1)S(1)}, bf16[64,2048]{1,0:T(8,128)(2,1)S(1)}, u32[]{:S(2)}, u32[]{:S(2)}) collective-permute-start(bf16[64,2048]{1,0:T(8,128)(2,1)S(1)} %fusion), channel_id=1, source_target_pairs={{0,16},{1,17},{2,18},{3,19},{4,20},{5,21},{6,22},{7,23},{8,24},{9,... | collective-permute-start | bytes 786440 | tf_op jit(solution)/shard_map/ppermute | solution.py:13
  145.4 9.4 %all-to-all-start.5 = ((bf16[4,12,2048]{2,1,0:T(8,128)(2,1)}), bf16[4,12,2048]{2,1,0:T(8,128)(2,1)S(1)}, u32[]{:S(2)}, u32[]{:S(2)}) async-start(bf16[4,12,2048]{2,1,0:T(8,128)(2,1)} %reshape.558), calls=%async_computation.5 | async-start | bytes 524288 | tf_op jit(solution)/shard_map/all_to_all | solution.py:76
  155.5 9.4 %all-to-all-start.7 = ((bf16[4,12,2048]{2,1,0:T(8,128)(2,1)}), bf16[4,12,2048]{2,1,0:T(8,128)(2,1)S(1)}, u32[]{:S(2)}, u32[]{:S(2)}) async-start(bf16[4,12,2048]{2,1,0:T(8,128)(2,1)} %reshape.561), calls=%async_computation.7 | async-start | bytes 524288 | tf_op jit(solution)/shard_map/all_to_all | solution.py:76
  165.2 0.7 copy-start.3
  166.8 9.4 %all-to-all-start.2 = ((bf16[4,12,2048]{2,1,0:T(8,128)(2,1)}), bf16[4,12,2048]{2,1,0:T(8,128)(2,1)S(1)}, u32[]{:S(2)}, u32[]{:S(2)}) async-start(bf16[4,12,2048]{2,1,0:T(8,128)(2,1)} %reshape.554), calls=%async_computation.2 | async-start | bytes 524288 | tf_op jit(solution)/shard_map/all_to_all | solution.py:75
  170.3 65.5 %reduce-scatter.2.cloned.1.call-start = ((), (), s32[]{:S(2)}) async-start(), calls=%async_computation.9 | async-start | bytes 3604480 | tf_op jit(solution)/shard_map/reduce_scatter | solution.py:109
  176.3 2.1 copy-start.1
  176.3 2.6 %copy-start.12 = (f32[48]{0:T(128)S(1)}, f32[48]{0:T(128)}, u32[]{:S(2)}) copy-start(f32[48]{0:T(128)} %reshape.567) | copy-start | bytes 580
  181.1 1.4 copy-start
  182.5 8.9 %copy-start.4 = (bf16[64,2048]{1,0:T(8,128)(2,1)S(1)}, bf16[64,2048]{1,0:T(8,128)(2,1)}, u32[]{:S(2)}) copy-start(bf16[64,2048]{1,0:T(8,128)(2,1)} %copy-done.3) | copy-start | bytes 786436
  182.5 9.5 %copy-start.6 = (bf16[64,2048]{1,0:T(8,128)(2,1)S(1)}, bf16[64,2048]{1,0:T(8,128)(2,1)}, u32[]{:S(2)}) copy-start(bf16[64,2048]{1,0:T(8,128)(2,1)} %copy-done.5) | copy-start | bytes 786436
Sparse Core Ops, SparseCore 0:
  9.6 37.4 all-gather.6
  48.6 33.8 all-gather.8
  84.0 33.7 all-gather.10
  181.3 54.3 reduce-scatter.1
where the time goes:
time: 243 us; the launch traced here: 242 us
  waiting for transfers between devices  166 us (68%)
  starting transfers between devices  28 us (12%)
  matrix products  14.2 us (6%)
  between operations  14.2 us (6%)
  blocking collectives  8.39 us (3%)
  local copies, waits for them, and re-layouts  8.09 us (3%)
  other arithmetic  3.92 us (2%)
    reduce_scatter x1, waiting for transfers between devices, local(): lax.psum_scatter(grad_total, 'dp', scatter_dimension=1, tiled=True)  42.8 us
    all_gather x1, waiting for transfers between devices, local(): lax.all_gather(w_up[0], 'dp', axis=1, tiled=True)  33.5 us
    all_gather x1, waiting for transfers between devices, local(): lax.all_gather(w_down[0], 'dp', axis=1, tiled=True)  33.4 us
    all_gather x1, waiting for transfers between devices, local(): lax.all_gather(w_gate[0], 'dp', axis=1, tiled=True)  24.1 us
    all_to_all x2, waiting for transfers between devices, local(): lax.all_to_all(send_cot, 'expert', split_axis=0, concat_axis=0, tiled=True)  10.9 us
    all_to_all x2, waiting for transfers between devices, local(): lax.all_to_all(send_tok, 'expert', split_axis=0, concat_axis=0, tiled=True)  9.79 us
    all_to_all x1, blocking collectives, local(): lax.all_to_all(partial_value, 'expert', split_axis=0, concat_axis=0, tile...  8.39 us
    all_to_all x2, starting transfers between devices, local(): lax.all_to_all(send_tok, 'expert', split_axis=0, concat_axis=0, tiled=True)  7.67 us
  transfers between devices with their start and end apart: 12, of which 11 were waited for; matrix products, arithmetic and copies ran while one was open for 6% of the time, Pallas kernels for 0%

commit v1 on v0

--- a/solution.py
+++ b/solution.py
@@ -1,3 +1,4 @@
+import functools
 import jax
 import jax.numpy as jnp
 from jax import lax
@@ -5,6 +6,14 @@
 
 SPLIT = 4
 CAP = 12
+
+
+def attach_skins(message, mesh_ax):
+    passed = jax.lax.all_gather(message, mesh_ax)
+    return jnp.concatenate(passed, axis=1)
+
+
+show_types = functools.partial(attach_skins, mesh_ax="dp")
 
 
 def shifted_2(shard, axis, by):
@@ -22,7 +31,7 @@
     step_count = routes.shape[1]
     gains = norm_gain[0]
     gate_local, up_local, down_local = (
-        lax.all_gather(w_gate[0], "dp", axis=1, tiled=True),
+        show_types(w_gate[0]),
         lax.all_gather(w_up[0], "dp", axis=1, tiled=True),
         lax.all_gather(w_down[0], "dp", axis=1, tiled=True),
     )

time: 243 us -> 243 us (level)
    dot_general x2, matrix products: 3.95 us -> 1.12 us  [local(): lax.dot_general(flat_tok, gate_local, dims, preferred_element_type=jnp.fl...]
  transfers between devices with their start and end apart: 12 -> 12, of which waited for: 11 -> 10; matrix products, arithmetic and copies ran while one was open for 6% -> 7% of each run, Pallas kernels for 0% -> 0%
where the time goes in v1:
time: 243 us; the launch traced here: 242 us
  waiting for transfers between devices  164 us (67%)
  starting transfers between devices  28.7 us (12%)
  between operations  14.2 us (6%)
  matrix products  13 us (5%)
  local copies, waits for them, and re-layouts  10.2 us (4%)
  blocking collectives  8.39 us (3%)
  other arithmetic  3.92 us (2%)
    reduce_scatter x1, waiting for transfers between devices, local(): lax.psum_scatter(grad_total, 'dp', scatter_dimension=1, tiled=True)  43.3 us
    all_gather x1, waiting for transfers between devices, local(): lax.all_gather(w_down[0], 'dp', axis=1, tiled=True)  33.4 us
    all_gather x1, waiting for transfers between devices, local(): lax.all_gather(w_up[0], 'dp', axis=1, tiled=True)  33.3 us
    all_gather x1, waiting for transfers between devices, attach_skins(): passed = jax.lax.all_gather(message, mesh_ax)  24 us
    all_to_all x2, waiting for transfers between devices, local(): lax.all_to_all(send_cot, 'expert', split_axis=0, concat_axis=0, tiled=True)  11 us
    all_to_all x1, blocking collectives, local(): lax.all_to_all(partial_value, 'expert', split_axis=0, concat_axis=0, tile...  8.39 us
    all_to_all x2, waiting for transfers between devices, local(): lax.all_to_all(send_tok, 'expert', split_axis=0, concat_axis=0, tiled=True)  8.09 us
    all_to_all x2, starting transfers between devices, local(): lax.all_to_all(send_tok, 'expert', split_axis=0, concat_axis=0, tiled=True)  7.67 us
  transfers between devices with their start and end apart: 12, of which 10 were waited for; matrix products, arithmetic and copies ran while one was open for 7% of the time, Pallas kernels for 0%

profile of v1, /device:TPU:0, one launch (start us, length us, event | category | flops | bytes accessed | tf_op | source)
XLA Modules:
  0.0 242.4 jit_solution(18441407254007996395)
XLA Ops:
  9.4 0.8 compare_reduce_fusion
  10.5 1.1 fusion.22
  11.9 0.7 reshape.556
  12.7 4.3 %all-to-all-start = ((bf16[4,12,2048]{2,1,0:T(8,128)(2,1)}), bf16[4,12,2048]{2,1,0:T(8,128)(2,1)S(1)}, u32[]{:S(2)}, u32[]{:S(2)}) async-start(bf16[4,12,2048]{2,1,0:T(8,128)(2,1)} %reshape.556), calls=%async_computation | async-start | bytes 524288 | tf_op jit(solution)/shard_map/all_to_all | solution.py:84
  17.7 5.3 %all-to-all-done = bf16[4,12,2048]{2,1,0:T(8,128)(2,1)S(1)} async-done(((bf16[4,12,2048]{2,1,0:T(8,128)(2,1)}), bf16[4,12,2048]{2,1,0:T(8,128)(2,1)S(1)}, u32[]{:S(2)}, u32[]{:S(2)}) %all-to-all-start) | async-done | bytes 196640 | tf_op jit(solution)/shard_map/all_to_all | solution.py:84
  23.0 24.0 %all-gather.6.cloned.1.call-done = bf16[4,352,512]{2,1,0:T(8,128)(2,1)} async-done(((bf16[1,352,512]{2,1,0:T(8,128)(2,1)}), bf16[4,352,512]{2,1,0:T(8,128)(2,1)}) %all-gather.6.cloned.1.call-update) | async-done | bytes 1441808 | tf_op jit(solution)/shard_map/all_gather | solution.py:12
  47.0 1.5 copy.22
  49.2 33.3 %all-gather.8.cloned.1.call-done = bf16[1,352,2048]{2,1,0:T(8,128)(2,1)} async-done(((bf16[1,352,512]{2,1,0:T(8,128)(2,1)}), bf16[1,352,2048]{2,1,0:T(8,128)(2,1)}) %all-gather.8.cloned.1.call-update) | async-done | bytes 1441808 | tf_op jit(solution)/shard_map/all_gather | solution.py:35
  82.5 1.9 fusion.18
  84.4 33.4 %all-gather.10.cloned.1.call-done = bf16[1,352,2048]{2,1,0:T(8,128)(2,1)} async-done(((bf16[1,352,512]{2,1,0:T(8,128)(2,1)}), bf16[1,352,2048]{2,1,0:T(8,128)(2,1)}) %all-gather.10.cloned.1.call-update) | async-done | bytes 1441808 | tf_op jit(solution)/shard_map/all_gather | solution.py:36
  117.8 1.7 convolution_convert_fusion.1
  119.5 0.8 reshape.560
  120.3 3.4 %all-to-all-start.1 = ((bf16[4,12,2048]{2,1,0:T(8,128)(2,1)}), bf16[4,12,2048]{2,1,0:T(8,128)(2,1)S(1)}, u32[]{:S(2)}, u32[]{:S(2)}) async-start(bf16[4,12,2048]{2,1,0:T(8,128)(2,1)} %reshape.560), calls=%async_computation.1 | async-start | bytes 524288 | tf_op jit(solution)/shard_map/all_to_all | solution.py:109
  123.9 5.8 %all-to-all-done.1 = bf16[4,12,2048]{2,1,0:T(8,128)(2,1)S(1)} async-done(((bf16[4,12,2048]{2,1,0:T(8,128)(2,1)}), bf16[4,12,2048]{2,1,0:T(8,128)(2,1)S(1)}, u32[]{:S(2)}, u32[]{:S(2)}) %all-to-all-start.1) | async-done | bytes 196640 | tf_op jit(solution)/shard_map/all_to_all | solution.py:109
  130.3 3.2 %all-to-all-start.4 = ((bf16[4,1,12]{2,1,0:T(2,128)(2,1)}), bf16[4,1,12]{2,1,0:T(2,128)(2,1)S(1)}, u32[]{:S(2)}, u32[]{:S(2)}) async-start(bf16[4,1,12]{2,1,0:T(2,128)(2,1)} %reshape.565), calls=%async_computation.4 | async-start | bytes 4096 | tf_op jit(solution)/shard_map/all_to_all | solution.py:86
  134.2 3.0 %all-to-all-done.4 = bf16[4,1,12]{2,1,0:T(2,128)(2,1)S(1)} async-done(((bf16[4,1,12]{2,1,0:T(2,128)(2,1)}), bf16[4,1,12]{2,1,0:T(2,128)(2,1)S(1)}, u32[]{:S(2)}, u32[]{:S(2)}) %all-to-all-start.4) | async-done | bytes 128 | tf_op jit(solution)/shard_map/all_to_all | solution.py:86
  137.8 3.2 %all-to-all-start.6 = ((bf16[4,1,12]{2,1,0:T(2,128)(2,1)}), bf16[4,1,12]{2,1,0:T(2,128)(2,1)S(1)}, u32[]{:S(2)}, u32[]{:S(2)}) async-start(bf16[4,1,12]{2,1,0:T(2,128)(2,1)} %reshape.568), calls=%async_computation.6 | async-start | bytes 4096 | tf_op jit(solution)/shard_map/all_to_all | solution.py:86
  141.0 4.2 %collective-permute-start = (bf16[64,2048]{1,0:T(8,128)(2,1)S(1)}, bf16[64,2048]{1,0:T(8,128)(2,1)}, u32[]{:S(2)}, u32[]{:S(2)}) collective-permute-start(bf16[64,2048]{1,0:T(8,128)(2,1)S(1)} %fusion), channel_id=1, source_target_pairs={{0,16},{1,17},{2,18},{3,19},{4,20},{5,21},{6,22},{7,23},{8,24},{9,... | collective-permute-start | bytes 786440 | tf_op jit(solution)/shard_map/ppermute | solution.py:22
  145.2 0.7 reshape.566
  145.9 3.4 %all-to-all-start.5 = ((bf16[4,12,2048]{2,1,0:T(8,128)(2,1)}), bf16[4,12,2048]{2,1,0:T(8,128)(2,1)S(1)}, u32[]{:S(2)}, u32[]{:S(2)}) async-start(bf16[4,12,2048]{2,1,0:T(8,128)(2,1)} %reshape.566), calls=%async_computation.5 | async-start | bytes 524288 | tf_op jit(solution)/shard_map/all_to_all | solution.py:85
  149.5 5.8 %all-to-all-done.5 = bf16[4,12,2048]{2,1,0:T(8,128)(2,1)S(1)} async-done(((bf16[4,12,2048]{2,1,0:T(8,128)(2,1)}), bf16[4,12,2048]{2,1,0:T(8,128)(2,1)S(1)}, u32[]{:S(2)}, u32[]{:S(2)}) %all-to-all-start.5) | async-done | bytes 196640 | tf_op jit(solution)/shard_map/all_to_all | solution.py:85
  156.0 3.4 %all-to-all-start.7 = ((bf16[4,12,2048]{2,1,0:T(8,128)(2,1)}), bf16[4,12,2048]{2,1,0:T(8,128)(2,1)S(1)}, u32[]{:S(2)}, u32[]{:S(2)}) async-start(bf16[4,12,2048]{2,1,0:T(8,128)(2,1)} %reshape.569), calls=%async_computation.7 | async-start | bytes 524288 | tf_op jit(solution)/shard_map/all_to_all | solution.py:85
  160.2 5.2 %all-to-all-done.7 = bf16[4,12,2048]{2,1,0:T(8,128)(2,1)S(1)} async-done(((bf16[4,12,2048]{2,1,0:T(8,128)(2,1)}), bf16[4,12,2048]{2,1,0:T(8,128)(2,1)S(1)}, u32[]{:S(2)}, u32[]{:S(2)}) %all-to-all-start.7) | async-done | bytes 196640 | tf_op jit(solution)/shard_map/all_to_all | solution.py:85
  166.7 0.7 reshape.562
  167.4 3.4 %all-to-all-start.2 = ((bf16[4,12,2048]{2,1,0:T(8,128)(2,1)}), bf16[4,12,2048]{2,1,0:T(8,128)(2,1)S(1)}, u32[]{:S(2)}, u32[]{:S(2)}) async-start(bf16[4,12,2048]{2,1,0:T(8,128)(2,1)} %reshape.562), calls=%async_computation.2 | async-start | bytes 524288 | tf_op jit(solution)/shard_map/all_to_all | solution.py:84
  170.9 3.1 %fusion.39 = f32[352,2048]{1,0:T(8,128)} fusion(bf16[48,2048]{1,0:T(8,128)(2,1)S(1)} %reshape.567, bf16[48,352]{1,0:T(8,128)(2,1)} %copy-done.9, f32[48]{0:T(128)S(1)} %reshape.574), kind=kOutput, calls=%fused_computation.48 | convolution fusion | flops 69256704 | bytes 3114176 | tf_op jit(solution)/shard_map/dot_general | solution.py:104
  174.0 2.8 %all-to-all-done.2 = bf16[4,12,2048]{2,1,0:T(8,128)(2,1)S(1)} async-done(((bf16[4,12,2048]{2,1,0:T(8,128)(2,1)}), bf16[4,12,2048]{2,1,0:T(8,128)(2,1)S(1)}, u32[]{:S(2)}, u32[]{:S(2)}) %all-to-all-start.2) | async-done | bytes 196640 | tf_op jit(solution)/shard_map/all_to_all | solution.py:84
  178.7 2.2 convolution_add_fusion
  180.9 1.3 copy-done.1
  182.6 8.4 %all_to_all.42 = bf16[4,12,2048]{2,1,0:T(8,128)(2,1)S(1)} all-to-all(bf16[4,12,2048]{2,1,0:T(8,128)(2,1)S(1)} %reshape.564), channel_id=1, replica_groups=mesh['section'=2,'expert'=4,'dp'=4] {'expert'}, dimensions={0} | all-to-all | bytes 393216 | tf_op jit(solution)/shard_map/all_to_all | solution.py:109
  191.8 0.8 maximum_bitcast_fusion
  192.6 43.3 %reduce-scatter.2.cloned.1.call-done = f32[352,512]{1,0:T(8,128)} async-done(((f32[352,2048]{1,0:T(8,128)}), f32[352,512]{1,0:T(8,128)}) %reduce-scatter.2.cloned.1.call-update) | async-done | bytes 720912 | tf_op jit(solution)/shard_map/reduce_scatter | solution.py:118
  (81 shorter events, 11.9 us)
Async XLA Ops:
  7.2 10.1 %copy-start.11 = (s32[1,2,64,6]{2,1,3,0:T(2,128)S(1)}, s32[1,2,64,6]{2,1,3,0:T(2,128)}, u32[]{:S(2)}) copy-start(s32[1,2,64,6]{2,1,3,0:T(2,128)} %param.11) | copy-start | bytes 9220
  7.2 4.5 %copy-start.3 = (bf16[1,64,2048]{2,1,0:T(8,128)(2,1)S(1)}, bf16[1,64,2048]{2,1,0:T(8,128)(2,1)}, u32[]{:S(2)}) copy-start(bf16[1,64,2048]{2,1,0:T(8,128)(2,1)} %param.9) | copy-start | bytes 786436
  7.2 4.5 %copy-start.14 = (f32[1,2048]{1,0:T(1,128)S(1)}, f32[1,2048]{1,0:T(1,128)}, u32[]{:S(2)}) copy-start(f32[1,2048]{1,0:T(1,128)} %param.14) | copy-start | bytes 24580
  7.2 10.1 %copy-start.12 = (bf16[1,2,64,6]{2,1,3,0:T(2,128)(2,1)S(1)}, bf16[1,2,64,6]{2,1,3,0:T(2,128)(2,1)}, u32[]{:S(2)}) copy-start(bf16[1,2,64,6]{2,1,3,0:T(2,128)(2,1)} %param.12) | copy-start | bytes 4612
  7.2 39.8 %all-gather.6.cloned.1.call-start = ((), (), s32[]{:S(2)}) async-start(), calls=%async_computation.9 | async-start | bytes 1802240 | tf_op jit(solution)/shard_map/all_gather | solution.py:12
  7.9 74.5 %all-gather.8.cloned.1.call-start = ((), (), s32[]{:S(2)}) async-start(), calls=%async_computation.11 | async-start | bytes 1802240 | tf_op jit(solution)/shard_map/all_gather | solution.py:35
  8.7 109.1 %all-gather.10.cloned.1.call-start = ((), (), s32[]{:S(2)}) async-start(), calls=%async_computation.12 | async-start | bytes 1802240 | tf_op jit(solution)/shard_map/all_gather | solution.py:36
  12.7 10.3 %all-to-all-start = ((bf16[4,12,2048]{2,1,0:T(8,128)(2,1)}), bf16[4,12,2048]{2,1,0:T(8,128)(2,1)S(1)}, u32[]{:S(2)}, u32[]{:S(2)}) async-start(bf16[4,12,2048]{2,1,0:T(8,128)(2,1)} %reshape.556), calls=%async_computation | async-start | bytes 524288 | tf_op jit(solution)/shard_map/all_to_all | solution.py:84
  84.4 35.9 %copy-start.9 = (bf16[48,352]{1,0:T(8,128)(2,1)}, bf16[48,352]{1,0:T(8,128)(2,1)S(1)}, u32[]{:S(2)}) copy-start(bf16[48,352]{1,0:T(8,128)(2,1)S(1)} %fusion.18) | copy-start | bytes 101380
  84.4 39.3 %copy-start.8 = (bf16[1,2,64,2048]{3,2,1,0:T(8,128)(2,1)S(1)}, bf16[1,2,64,2048]{3,2,1,0:T(8,128)(2,1)}, u32[]{:S(2)}) copy-start(bf16[1,2,64,2048]{3,2,1,0:T(8,128)(2,1)} %param.13) | copy-start | bytes 1572868
  120.3 9.4 %all-to-all-start.1 = ((bf16[4,12,2048]{2,1,0:T(8,128)(2,1)}), bf16[4,12,2048]{2,1,0:T(8,128)(2,1)S(1)}, u32[]{:S(2)}, u32[]{:S(2)}) async-start(bf16[4,12,2048]{2,1,0:T(8,128)(2,1)} %reshape.560), calls=%async_computation.1 | async-start | bytes 524288 | tf_op jit(solution)/shard_map/all_to_all | solution.py:109
  130.3 6.9 %all-to-all-start.4 = ((bf16[4,1,12]{2,1,0:T(2,128)(2,1)}), bf16[4,1,12]{2,1,0:T(2,128)(2,1)S(1)}, u32[]{:S(2)}, u32[]{:S(2)}) async-start(bf16[4,1,12]{2,1,0:T(2,128)(2,1)} %reshape.565), calls=%async_computation.4 | async-start | bytes 4096 | tf_op jit(solution)/shard_map/all_to_all | solution.py:86
  134.2 31.3 %copy-start.6 = (bf16[64,2048]{1,0:T(8,128)(2,1)}, bf16[64,2048]{1,0:T(8,128)(2,1)S(1)}, u32[]{:S(2)}) copy-start(bf16[64,2048]{1,0:T(8,128)(2,1)S(1)} %fusion) | copy-start | bytes 786436
  137.8 7.4 %all-to-all-start.6 = ((bf16[4,1,12]{2,1,0:T(2,128)(2,1)}), bf16[4,1,12]{2,1,0:T(2,128)(2,1)S(1)}, u32[]{:S(2)}, u32[]{:S(2)}) async-start(bf16[4,1,12]{2,1,0:T(2,128)(2,1)} %reshape.568), calls=%async_computation.6 | async-start | bytes 4096 | tf_op jit(solution)/shard_map/all_to_all | solution.py:86
  141.0 24.5 %copy-start.10 = (bf16[1,64,2048]{2,1,0:T(8,128)(2,1)S(1)}, bf16[1,64,2048]{2,1,0:T(8,128)(2,1)}, u32[]{:S(2)}) copy-start(bf16[1,64,2048]{2,1,0:T(8,128)(2,1)} %param.10) | copy-start | bytes 786436
  141.0 24.5 %collective-permute-start = (bf16[64,2048]{1,0:T(8,128)(2,1)S(1)}, bf16[64,2048]{1,0:T(8,128)(2,1)}, u32[]{:S(2)}, u32[]{:S(2)}) collective-permute-start(bf16[64,2048]{1,0:T(8,128)(2,1)S(1)} %fusion), channel_id=1, source_target_pairs={{0,16},{1,17},{2,18},{3,19},{4,20},{5,21},{6,22},{7,23},{8,24},{9,... | collective-permute-start | bytes 786440 | tf_op jit(solution)/shard_map/ppermute | solution.py:22
  145.9 9.4 %all-to-all-start.5 = ((bf16[4,12,2048]{2,1,0:T(8,128)(2,1)}), bf16[4,12,2048]{2,1,0:T(8,128)(2,1)S(1)}, u32[]{:S(2)}, u32[]{:S(2)}) async-start(bf16[4,12,2048]{2,1,0:T(8,128)(2,1)} %reshape.566), calls=%async_computation.5 | async-start | bytes 524288 | tf_op jit(solution)/shard_map/all_to_all | solution.py:85
  156.0 9.4 %all-to-all-start.7 = ((bf16[4,12,2048]{2,1,0:T(8,128)(2,1)}), bf16[4,12,2048]{2,1,0:T(8,128)(2,1)S(1)}, u32[]{:S(2)}, u32[]{:S(2)}) async-start(bf16[4,12,2048]{2,1,0:T(8,128)(2,1)} %reshape.569), calls=%async_computation.7 | async-start | bytes 524288 | tf_op jit(solution)/shard_map/all_to_all | solution.py:85
  165.7 0.7 copy-start.4
  167.4 9.4 %all-to-all-start.2 = ((bf16[4,12,2048]{2,1,0:T(8,128)(2,1)}), bf16[4,12,2048]{2,1,0:T(8,128)(2,1)S(1)}, u32[]{:S(2)}, u32[]{:S(2)}) async-start(bf16[4,12,2048]{2,1,0:T(8,128)(2,1)} %reshape.562), calls=%async_computation.2 | async-start | bytes 524288 | tf_op jit(solution)/shard_map/all_to_all | solution.py:84
  170.8 65.0 %reduce-scatter.2.cloned.1.call-start = ((), (), s32[]{:S(2)}) async-start(), calls=%async_computation.10 | async-start | bytes 3604480 | tf_op jit(solution)/shard_map/reduce_scatter | solution.py:118
  170.9 6.6 %copy-start.2 = (bf16[1,352,2048]{2,1,0:T(8,128)(2,1)S(1)}, bf16[1,352,2048]{2,1,0:T(8,128)(2,1)}, u32[]{:S(2)}) copy-start(bf16[1,352,2048]{2,1,0:T(8,128)(2,1)} %all-gather.8.cloned.1.call-done) | copy-start | bytes 4325380
  176.8 1.8 copy-start
  176.8 1.8 copy-start.13
  180.9 1.4 copy-start.1
  182.2 8.9 %copy-start.5 = (bf16[64,2048]{1,0:T(8,128)(2,1)S(1)}, bf16[64,2048]{1,0:T(8,128)(2,1)}, u32[]{:S(2)}) copy-start(bf16[64,2048]{1,0:T(8,128)(2,1)} %copy-done.4) | copy-start | bytes 786436
  182.2 9.5 %copy-start.7 = (bf16[64,2048]{1,0:T(8,128)(2,1)S(1)}, bf16[64,2048]{1,0:T(8,128)(2,1)}, u32[]{:S(2)}) copy-start(bf16[64,2048]{1,0:T(8,128)(2,1)} %copy-done.6) | copy-start | bytes 786436
Sparse Core Ops, SparseCore 0:
  9.6 37.4 all-gather.5
  48.6 33.8 all-gather.7
  84.0 33.7 all-gather.9
  181.0 54.8 reduce-scatter.1
